TPU v7x, 256 devices: a whole 4x4x8 slice. The times are simulated.
256 devices in a mesh: section: 8 (over x, core), paths: 32 (over y, z).
Axes of the slice: x: 4, y: 4, z: 8, core: 2. Of those that a mesh axis runs over, the one named last changes fastest.
Arguments:
- normal_draws: float32 [16, 60, 32768], P('section', None, 'paths'), may hold values from -6 to 6
- cholesky: float32 [16, 32, 60, 60], P('section', 'paths'), as said below
- log_spot: float32 [60], replicated, may hold values from -0.2 to 0.2
- owner: int32 [16], replicated, may hold values from 0 to 31
- trade_factor: int32 [4096], replicated, may hold values from 0 to 59
- trade_set: int32 [4096], replicated, may hold values from 0 to 511
- notional: float32 [4096], replicated, may hold values from -5 to 5
- strike: float32 [4096], replicated, may hold values from 0.8 to 1.25
Outputs:
- exposure: float32 [16, 512], P('section')
Inputs may be any that keep to these rules, and one draw needn't show every extreme that they name: `cholesky`: each block is lower triangular with a positive diagonal.
All inputs are finite; a program needn't handle non-finite values.
Results may differ from a plain program's by a relative error of at most 0.0001.
Values sent between devices are 32-bit elements; how exact they have to be, the bound alone decides.
A program may use at most 64 MiB of HBM per device.

v0:
```python
import functools

import jax
import jax.numpy as jnp
from jax import lax
from jax.experimental import pallas as pl
from jax.experimental.pallas import tpu as pltpu
from jax.sharding import PartitionSpec as P

SETS = 512
TRADES = 4096
LANES = 128
ROWS = TRADES // LANES
HALF = TRADES // 2
MESH = pl.DeviceIdType.MESH
HIGHEST = lax.Precision.HIGHEST
F32 = jnp.float32
I32 = jnp.int32


def iota(shape, axis):
    return lax.broadcasted_iota(I32, shape, axis)


def remote(src, dst, send, recv, device):
    return pltpu.make_async_remote_copy(
        src_ref=src, dst_ref=dst, send_sem=send, recv_sem=recv, device_id=device, device_id_type=MESH
    )


def packed(first, second):
    row, col = iota((64, LANES), 0), iota((64, LANES), 1)
    across = jnp.transpose(second)[:64]
    square = jnp.where(col <= row, first[:64], across)
    diagonal = jnp.sum(jnp.where(col == row, second[:64], 0.0), axis=0, keepdims=True)
    square = jnp.where(row == 60, diagonal, square)
    return jnp.where(col[:32] < 64, square[:32], pltpu.roll(square[32:], 64, 1))


def unpacked(both):
    row, col = iota((64, LANES), 0), iota((64, LANES), 1)
    square = jnp.concatenate([both, pltpu.roll(both, 64, 1)], axis=0)
    square = jnp.where(col < 64, square, 0.0)
    first = jnp.where((col <= row) & (row < 60), square, 0.0)
    across = jnp.transpose(jnp.concatenate([square, jnp.zeros_like(square)], axis=0))[:64]
    second = jnp.where(col < row, across, 0.0)
    second = jnp.where(col == row, square[60:61], second)
    return first, jnp.where(row < 60, second, 0.0)


def partner(x, bit):
    if bit < 2:
        step = 1 << bit
        return [x[place ^ step] for place in range(4)]
    axis, step, extent = (0, 1 << (bit - 2), 8) if bit < 5 else (1, 1 << (bit - 5), LANES)
    upper = (iota((8, LANES), axis) & step) != 0
    return [
        jnp.where(upper, pltpu.roll(v, step, axis), pltpu.roll(v, extent - step, axis)) for v in x
    ]


def place_bit(bit, vreg):
    if bit < 2:
        return jnp.full((8, LANES), (vreg >> bit) & 1, I32)
    axis, shift = (0, bit - 2) if bit < 5 else (1, bit - 5)
    return (iota((8, LANES), axis) >> shift) & 1


def in_set_order(keys, carried):
    for level in range(1, 13):
        for bit in range(level - 1, -1, -1):
            other = partner(keys, bit)
            others = [partner(c, bit) for c in carried]
            new_keys, news = [], [[] for _ in carried]
            for v in range(4):
                upward = place_bit(level, v) if level < 12 else jnp.zeros((8, LANES), I32)
                wants_small = place_bit(bit, v) == upward
                swap = jnp.where(wants_small, keys[v] - other[v], other[v] - keys[v]) > 0
                new_keys.append(jnp.where(swap, other[v], keys[v]))
                for new, c, o in zip(news, carried, others):
                    new.append(jnp.where(swap, o[v], c[v]))
            keys, carried = new_keys, news
    return keys, carried


def kernel(
    sections, ys, zs, factors,
    draws, chol, spot, owner, tfactor, tset, notional, strike, out,
    chol_in, spot_in, owner_in, trades_in, trades_f_in, pack_a, pack_b,
    mine, over_y, y_sum, over_z, blocks, z_all, prices, order, order_in, ends, ends_in,
    strikes, notionals, keeps, nets, sums, over_x, x_sum, over_fy, fy_sum, over_fz,
    in_sems, order_sem, ends_sem, own_sem, y_send, y_recv, z_send, z_recv, x_send, x_recv,
    d_send, d_recv, fx_send, fx_recv, fy_send, fy_recv, fz_send, fz_recv,
):
    dates = 2 * sections
    section = lax.axis_index("section")
    place = lax.axis_index("paths")
    y, z = lax.div(place, zs), lax.rem(place, zs)
    y_peers = [(section, lax.rem(y + i, ys) * zs + z) for i in range(1, ys)]
    z_peers = [(section, y * zs + lax.rem(z + i, zs)) for i in range(1, zs)]
    x_peers = [(lax.rem(section + i, sections), place) for i in range(1, sections)]

    barrier = pltpu.get_barrier_semaphore()
    for peer in y_peers + z_peers + x_peers:
        pl.semaphore_signal(barrier, inc=1, device_id=peer, device_id_type=MESH)

    loads = [
        pltpu.make_async_copy(chol, chol_in, in_sems.at[0]),
        pltpu.make_async_copy(owner, owner_in, in_sems.at[1]),
        pltpu.make_async_copy(spot, spot_in, in_sems.at[2]),
        pltpu.make_async_copy(tfactor, trades_in.at[0], in_sems.at[3]),
        pltpu.make_async_copy(tset, trades_in.at[1], in_sems.at[4]),
        pltpu.make_async_copy(notional, trades_f_in.at[0], in_sems.at[5]),
        pltpu.make_async_copy(strike, trades_f_in.at[1], in_sems.at[6]),
    ]
    for load in loads:
        load.start()
    own = pltpu.make_async_copy(
        draws.at[:, :, pl.ds(pl.multiple_of(section * LANES, LANES), LANES)],
        z_all.at[section, :, pl.ds(0, factors), :],
        own_sem,
    )
    own.start()

    pack_a[...] = jnp.zeros_like(pack_a)
    pack_b[...] = jnp.zeros_like(pack_b)
    for e in range(sections):
        for d in range(2):
            z_all[e, d, factors:64, :] = jnp.zeros((64 - factors, LANES), F32)
    loads[0].wait()
    loads[1].wait()
    pack_a[0:factors, 0:factors] = jnp.where(owner_in[2 * section] == place, chol_in[0], 0.0)
    pack_b[0:factors, 0:factors] = jnp.where(owner_in[2 * section + 1] == place, chol_in[1], 0.0)
    mine[...] = packed(pack_a[...], pack_b[...])

    pl.semaphore_wait(barrier, len(y_peers) + len(z_peers) + len(x_peers))

    to_y = [
        remote(mine, over_y.at[i], y_send.at[i], y_recv.at[i], peer) for i, peer in enumerate(y_peers)
    ]
    for copy in to_y:
        copy.start()
    to_d = [
        remote(
            draws.at[:, :, pl.ds(pl.multiple_of(peer[0] * LANES, LANES), LANES)],
            z_all.at[section, :, pl.ds(0, factors), :],
            d_send.at[i], d_recv.at[i], peer,
        )
        for i, peer in enumerate(x_peers)
    ]
    for copy in to_d:
        copy.start()

    for load in loads[2:]:
        load.wait()
    keys = [
        trades_in[1, 8 * v:8 * v + 8, :] * 64 + trades_in[0, 8 * v:8 * v + 8, :] for v in range(4)
    ]
    carried = [[trades_f_in[a, 8 * v:8 * v + 8, :] for v in range(4)] for a in range(2)]
    keys, (notional_s, strike_s) = in_set_order(keys, carried)
    for v in range(4):
        order[8 * v:8 * v + 8, :] = keys[v] & 63
    to_order = pltpu.make_async_copy(order, order_in, order_sem)
    to_order.start()

    total = mine[...]
    for i, copy in enumerate(to_y):
        copy.wait_recv()
        total = total + over_y[i]
    y_sum[...] = total
    to_z = [
        remote(y_sum, over_z.at[i], z_send.at[i], z_recv.at[i], peer) for i, peer in enumerate(z_peers)
    ]
    for copy in to_z:
        copy.start()

    set_s = [k >> 6 for k in keys]
    sub, lane = iota((8, LANES), 0), iota((8, LANES), 1)
    down = pltpu.roll(set_s[3], 1, 0)
    before = [jnp.where(sub == 0, pltpu.roll(down, 1, 1), down), set_s[0], set_s[1], set_s[2]]
    keep_s = []
    for v in range(4):
        same = jnp.where(before[v] == set_s[v], 1.0, 0.0)
        if v == 0:
            same = jnp.where((sub == 0) & ((lane == 0) | (lane == LANES // 2)), 0.0, same)
        keep_s.append(same)
    for c in range(LANES):
        for v in range(4):
            at = pl.ds(c * 32 + 8 * v, 8)
            strikes[at, :] = jnp.broadcast_to(strike_s[v][:, c:c + 1], (8, LANES))
            notionals[at, :] = jnp.broadcast_to(notional_s[v][:, c:c + 1], (8, LANES))
            keeps[at, :] = jnp.broadcast_to(keep_s[v][:, c:c + 1], (8, LANES))

    counts = jnp.zeros((8, LANES), F32)
    low = iota((LANES, LANES), 0)
    for r in range(ROWS):
        sets = trades_in[1, r:r + 1, :]
        fine = jnp.where((sets & 127) == low, 1.0, 0.0)
        coarse = jnp.where((sets >> 7) == sub, 1.0, 0.0)
        counts = counts + lax.dot_general(
            coarse, fine, (((1,), (1,)), ((), ())), preferred_element_type=F32
        )
    upto = jnp.where(low <= iota((LANES, LANES), 1), 1.0, 0.0)
    through = jnp.dot(counts, upto, precision=HIGHEST, preferred_element_type=F32)
    offset = jnp.zeros((8, 1), F32)
    for h in range(SETS // LANES - 1):
        offset = offset + jnp.where(iota((8, 1), 0) > h, through[h:h + 1, LANES - 1:], 0.0)
    through = (through + offset).astype(I32)
    counts = counts.astype(I32)
    ends[0] = jnp.where(counts > 0, through - 1, TRADES)
    ends[1] = jnp.where((through - counts < HALF) & (through > HALF), HALF - 1, TRADES)
    to_ends = pltpu.make_async_copy(ends, ends_in, ends_sem)
    to_ends.start()

    spots = jnp.concatenate([spot_in[...], jnp.zeros((1, LANES - factors), F32)], axis=1)
    level = jnp.transpose(jnp.broadcast_to(spots, (LANES, LANES)))[:64]
    nets[TRADES] = jnp.zeros((dates, LANES), F32)

    total = y_sum[...]
    for i, copy in enumerate(to_z):
        copy.wait_recv()
        total = total + over_z[i]
    blocks[section] = total
    to_x = [
        remote(blocks.at[section], blocks.at[section], x_send.at[i], x_recv.at[i], peer)
        for i, peer in enumerate(x_peers)
    ]
    for copy in to_x:
        copy.start()
    own.wait()
    to_order.wait()
    to_ends.wait()
    for copy in to_d:
        copy.wait_recv()
    for copy in to_x:
        copy.wait_recv()

    for e in range(sections):
        for d, lower in enumerate(unpacked(blocks[e])):
            level = level + jnp.dot(
                lower[:, :64], z_all[e, d], precision=HIGHEST, preferred_element_type=F32
            )
            prices[:, 2 * e + d, :] = jnp.exp(level)

    def some_trades(c, accs):
        accs = list(accs)
        for j in range(32):
            row = (j & 3) * 8 + (j >> 2)
            for half in range(2):
                column = c + half * (LANES // 2)
                at = pl.ds(column * 32 + row, 1)
                price = prices[order_in[row, column]]
                payoff = notionals[at, :] * jnp.maximum(price - strikes[at, :], 0.0)
                accs[half] = accs[half] * keeps[at, :] + payoff
                nets[column * 32 + j] = accs[half]
        return tuple(accs)

    zero = jnp.zeros((dates, LANES), F32)
    lax.fori_loop(0, LANES // 2, some_trades, (zero, zero))

    lanes = iota((dates, LANES), 1)
    step = 32
    for b in range(SETS // LANES):
        def some_sets(q, sums_b):
            for i in range(step):
                at = q * step + i
                last, halfway = (jnp.clip(ends_in[a, b, at], 0, TRADES) for a in range(2))
                net = nets[last] + nets[halfway]
                sum_s = jnp.sum(jnp.maximum(net, 0.0), axis=1, keepdims=True)
                sums_b = jnp.where(lanes == at, sum_s, sums_b)
            return sums_b

        sums_b = lax.fori_loop(0, LANES // step, some_sets, jnp.zeros((dates, LANES), F32))
        for d in range(dates):
            sums[4 * d + b:4 * d + b + 1, :] = sums_b[d:d + 1]

    def rows_of(s):
        return sums.at[pl.ds(pl.multiple_of(s * 8, 8), 8), :]

    to_fx = [
        remote(rows_of(peer[0]), over_x.at[i], fx_send.at[i], fx_recv.at[i], peer)
        for i, peer in enumerate(x_peers)
    ]
    for copy in to_fx:
        copy.start()
    total = sums[pl.ds(pl.multiple_of(section * 8, 8), 8), :]
    for i, copy in enumerate(to_fx):
        copy.wait_recv()
        total = total + over_x[i]
    x_sum[...] = total
    to_fy = [
        remote(x_sum, over_fy.at[i], fy_send.at[i], fy_recv.at[i], peer)
        for i, peer in enumerate(y_peers)
    ]
    for copy in to_fy:
        copy.start()
    for i, copy in enumerate(to_fy):
        copy.wait_recv()
        total = total + over_fy[i]
    fy_sum[...] = total
    to_fz = [
        remote(fy_sum, over_fz.at[i], fz_send.at[i], fz_recv.at[i], peer)
        for i, peer in enumerate(z_peers)
    ]
    for copy in to_fz:
        copy.start()
    for i, copy in enumerate(to_fz):
        copy.wait_recv()
        total = total + over_fz[i]
    out[...] = total
    for copies in (to_y, to_z, to_x, to_d, to_fx, to_fy, to_fz):
        for copy in copies:
            copy.wait_send()


def shards(sections, ys, zs, normal_draws, cholesky, log_spot, owner, trade_factor, trade_set, notional, strike):
    factors = normal_draws.shape[1]
    dates = 2 * sections
    dma = pltpu.SemaphoreType.DMA
    vmem = pltpu.VMEM
    square = (ROWS, LANES)
    totals = pl.pallas_call(
        functools.partial(kernel, sections, ys, zs, factors),
        out_shape=jax.ShapeDtypeStruct((8, LANES), F32),
        in_specs=[pl.BlockSpec(memory_space=pl.ANY)] * 8,
        out_specs=pl.BlockSpec(memory_space=pltpu.VMEM),
        scratch_shapes=[
            vmem((2, factors, factors), F32),
            vmem((1, factors), F32),
            pltpu.SMEM((dates,), I32),
            vmem((2, *square), I32),
            vmem((2, *square), F32),
            vmem((LANES, LANES), F32),
            vmem((LANES, LANES), F32),
            vmem((32, LANES), F32),
            vmem((ys - 1, 32, LANES), F32),
            vmem((32, LANES), F32),
            vmem((zs - 1, 32, LANES), F32),
            vmem((sections, 32, LANES), F32),
            vmem((sections, 2, 64, LANES), F32),
            vmem((64, dates, LANES), F32),
            vmem(square, I32),
            pltpu.SMEM(square, I32),
            vmem((2, 8, LANES), I32),
            pltpu.SMEM((2, 8, LANES), I32),
            vmem((TRADES, LANES), F32),
            vmem((TRADES, LANES), F32),
            vmem((TRADES, LANES), F32),
            vmem((TRADES + 1, dates, LANES), F32),
            vmem((4 * dates, LANES), F32),
            vmem((sections - 1, 8, LANES), F32),
            vmem((8, LANES), F32),
            vmem((ys - 1, 8, LANES), F32),
            vmem((8, LANES), F32),
            vmem((zs - 1, 8, LANES), F32),
            dma((7,)), dma, dma, dma,
            dma((ys - 1,)), dma((ys - 1,)), dma((zs - 1,)), dma((zs - 1,)),
            dma((sections - 1,)), dma((sections - 1,)), dma((sections - 1,)), dma((sections - 1,)),
            dma((sections - 1,)), dma((sections - 1,)), dma((ys - 1,)), dma((ys - 1,)),
            dma((zs - 1,)), dma((zs - 1,)),
        ],
        compiler_params=pltpu.CompilerParams(
            collective_id=0, has_side_effects=True, vmem_limit_bytes=60 * 1024 * 1024
        ),
    )(
        normal_draws, cholesky[:, 0], log_spot.reshape(1, factors), owner,
        trade_factor.reshape(square), trade_set.reshape(square),
        notional.reshape(square), strike.reshape(square),
    )
    paths = normal_draws.shape[2] * ys * zs
    return totals.reshape(2, SETS) / paths


def solution(mesh):
    placed = (
        P("section", None, "paths"),
        P("section", "paths", None, None),
        P(), P(), P(), P(), P(), P(),
    )
    sections, paths = mesh.shape["section"], mesh.shape["paths"]
    zs = 8 if paths == 32 else 2
    return jax.shard_map(
        functools.partial(shards, sections, paths // zs, zs),
        mesh=mesh, in_specs=placed, out_specs=P("section", None), check_vma=False,
    )
```

profile of v0, /device:TPU:1, one launch (start us, length us, event | category | flops | bytes accessed | tf_op | source)
XLA Modules:
  0.0 51.2 jit_solution(16437480346164843809)
XLA Ops:
  0.0 0.9 %copy.14 = f32[2,1,60,60]{3,0,2,1:T(2,128)S(1)} copy(f32[2,1,60,60]{3,1,2,0:T(1,128)} %param.9) | data formatting | bytes 57600 | tf_op args[1]
  0.9 0.6 %copy.12.chol = f32[2,60,60]{2,1,0:T(8,128)} copy(f32[2,60,60]{2,0,1:T(2,128)S(1)} %bitcast.8) | data formatting | bytes 57600 | tf_op jit(solution)/shard_map/squeeze | solution.py:366
  1.5 2.0 %copy.11.draws = f32[2,60,1024]{2,1,0:T(8,128)} copy(f32[2,60,1024]{2,0,1:T(2,128)} %param.8) | data formatting | bytes 983040 | tf_op args[0]
  3.5 46.5 %shard_map.82 = f32[8,128]{1,0:T(8,128)} custom-call(f32[2,60,1024]{2,1,0:T(8,128)} %copy.11.draws, f32[2,60,60]{2,1,0:T(8,128)} %copy.12.chol, f32[1,60]{1,0:T(1,128)} %bitcast.13, s32[16]{0:T(128)} %owner.1, s32[32,128]{1,0:T(8,128)} %bitcast.9, s32[32,128]{1,0:T(8,128)} %bitcast.10, f32[32,128]{1,0:T(8,128)} %bitcast.11, f32[32,128]{1,0:T(8,128)} %bitcast.12), custom_call_target="tpu_custom_call" | custom-call | tf_op jit(solution)/shard_map/pallas_call | solution.py:322
  49.9 0.7 %broadcast_multiply_fusion = f32[8,128]{1,0:T(8,128)S(1)} fusion(f32[8,128]{1,0:T(8,128)} %shard_map.82), kind=kLoop, calls=%fused_computation.1 | loop fusion | flops 1024 | bytes 8192 | tf_op jit(solution)/shard_map/div | solution.py:371
  50.6 0.6 %div.10 = f32[2,512]{1,0:T(2,128)} reshape(f32[8,128]{1,0:T(8,128)S(1)} %broadcast_multiply_fusion) | data formatting | bytes 8192 | tf_op jit(solution)/shard_map/div | solution.py:371
where the time goes:
time: 51.5 us; the launch traced here: 51.2 us
  Pallas kernels  46.5 us (90%)
  local copies, waits for them, and re-layouts  4.06 us (8%)
  other arithmetic  0.69 us (1%)
    pallas_call x1, Pallas kernels, shards(): pl.pallas_call(functools.partial(kernel, sections, ys, zs, factors), out_...  46.5 us
    unnamed x2, local copies, waits for them, and re-layouts  2.84 us

commit v1 on v0

--- a/solution.py
+++ b/solution.py
@@ -12,6 +12,7 @@
 LANES = 128
 ROWS = TRADES // LANES
 HALF = TRADES // 2
+CHUNKS = 2
 MESH = pl.DeviceIdType.MESH
 HIGHEST = lax.Precision.HIGHEST
 F32 = jnp.float32
@@ -46,6 +47,11 @@
     second = jnp.where(col < row, across, 0.0)
     second = jnp.where(col == row, square[60:61], second)
     return first, jnp.where(row < 60, second, 0.0)
+
+
+def halves(x):
+    high = x.astype(jnp.bfloat16).astype(F32)
+    return high, x - high
 
 
 def partner(x, bit):
@@ -84,11 +90,11 @@
 
 
 def kernel(
-    sections, ys, zs, factors,
+    sections, ys, zs, factors, paths,
     draws, chol, spot, owner, tfactor, tset, notional, strike, out,
     chol_in, spot_in, owner_in, trades_in, trades_f_in, pack_a, pack_b,
-    mine, over_y, y_sum, over_z, blocks, z_all, prices, order, order_in, ends, ends_in,
-    strikes, notionals, keeps, nets, sums, over_x, x_sum, over_fy, fy_sum, over_fz,
+    mine, over_y, y_sum, over_z, blocks, z_all, z_parts, prices, order, order_in, ends, ends_in,
+    strikes, notionals, keeps, floors, nets, sums, over_x, x_sum, over_fy, fy_sum, over_fz,
     in_sems, order_sem, ends_sem, own_sem, y_send, y_recv, z_send, z_recv, x_send, x_recv,
     d_send, d_recv, fx_send, fx_recv, fy_send, fy_recv, fz_send, fz_recv,
 ):
@@ -117,7 +123,7 @@
         load.start()
     own = pltpu.make_async_copy(
         draws.at[:, :, pl.ds(pl.multiple_of(section * LANES, LANES), LANES)],
-        z_all.at[section, :, pl.ds(0, factors), :],
+        z_all.at[section, pl.ds(0, factors)],
         own_sem,
     )
     own.start()
@@ -125,25 +131,32 @@
     pack_a[...] = jnp.zeros_like(pack_a)
     pack_b[...] = jnp.zeros_like(pack_b)
     for e in range(sections):
-        for d in range(2):
-            z_all[e, d, factors:64, :] = jnp.zeros((64 - factors, LANES), F32)
+        z_all[e, factors:64] = jnp.zeros((64 - factors, 2, LANES), F32)
     loads[0].wait()
     loads[1].wait()
-    pack_a[0:factors, 0:factors] = jnp.where(owner_in[2 * section] == place, chol_in[0], 0.0)
-    pack_b[0:factors, 0:factors] = jnp.where(owner_in[2 * section + 1] == place, chol_in[1], 0.0)
+    pack_a[0:factors, 0:factors] = jnp.where(owner_in[2 * section] == place, chol_in[0, :, 0, :], 0.0)
+    pack_b[0:factors, 0:factors] = jnp.where(owner_in[2 * section + 1] == place, chol_in[1, :, 0, :], 0.0)
     mine[...] = packed(pack_a[...], pack_b[...])
 
     pl.semaphore_wait(barrier, len(y_peers) + len(z_peers) + len(x_peers))
 
-    to_y = [
-        remote(mine, over_y.at[i], y_send.at[i], y_recv.at[i], peer) for i, peer in enumerate(y_peers)
-    ]
-    for copy in to_y:
-        copy.start()
+    def part(c):
+        return pl.ds(c * (32 // CHUNKS), 32 // CHUNKS)
+
+    def sends(peers, source, target, send, recv, c):
+        copies = [
+            remote(source.at[part(c)], target(i).at[part(c)], send.at[i, c], recv.at[i, c], peer)
+            for i, peer in enumerate(peers)
+        ]
+        for copy in copies:
+            copy.start()
+        return copies
+
+    to_y = [sends(y_peers, mine, lambda i: over_y.at[i], y_send, y_recv, c) for c in range(CHUNKS)]
     to_d = [
         remote(
             draws.at[:, :, pl.ds(pl.multiple_of(peer[0] * LANES, LANES), LANES)],
-            z_all.at[section, :, pl.ds(0, factors), :],
+            z_all.at[section, pl.ds(0, factors)],
             d_send.at[i], d_recv.at[i], peer,
         )
         for i, peer in enumerate(x_peers)
@@ -158,21 +171,19 @@
     ]
     carried = [[trades_f_in[a, 8 * v:8 * v + 8, :] for v in range(4)] for a in range(2)]
     keys, (notional_s, strike_s) = in_set_order(keys, carried)
-    for v in range(4):
-        order[8 * v:8 * v + 8, :] = keys[v] & 63
+    wide = jnp.concatenate([k & 63 for k in keys] * 4, axis=0)
+    order[...] = jnp.transpose(wide)
     to_order = pltpu.make_async_copy(order, order_in, order_sem)
     to_order.start()
 
-    total = mine[...]
-    for i, copy in enumerate(to_y):
-        copy.wait_recv()
-        total = total + over_y[i]
-    y_sum[...] = total
-    to_z = [
-        remote(y_sum, over_z.at[i], z_send.at[i], z_recv.at[i], peer) for i, peer in enumerate(z_peers)
-    ]
-    for copy in to_z:
-        copy.start()
+    to_z = []
+    for c in range(CHUNKS):
+        total = mine[part(c), :]
+        for i, copy in enumerate(to_y[c]):
+            copy.wait_recv()
+            total = total + over_y[i, part(c), :]
+        y_sum[part(c), :] = total
+        to_z.append(sends(z_peers, y_sum, lambda i: over_z.at[i], z_send, z_recv, c))
 
     set_s = [k >> 6 for k in keys]
     sub, lane = iota((8, LANES), 0), iota((8, LANES), 1)
@@ -191,54 +202,74 @@
             notionals[at, :] = jnp.broadcast_to(notional_s[v][:, c:c + 1], (8, LANES))
             keeps[at, :] = jnp.broadcast_to(keep_s[v][:, c:c + 1], (8, LANES))
 
-    counts = jnp.zeros((8, LANES), F32)
-    low = iota((LANES, LANES), 0)
-    for r in range(ROWS):
-        sets = trades_in[1, r:r + 1, :]
-        fine = jnp.where((sets & 127) == low, 1.0, 0.0)
-        coarse = jnp.where((sets >> 7) == sub, 1.0, 0.0)
-        counts = counts + lax.dot_general(
-            coarse, fine, (((1,), (1,)), ((), ())), preferred_element_type=F32
-        )
-    upto = jnp.where(low <= iota((LANES, LANES), 1), 1.0, 0.0)
-    through = jnp.dot(counts, upto, precision=HIGHEST, preferred_element_type=F32)
-    offset = jnp.zeros((8, 1), F32)
-    for h in range(SETS // LANES - 1):
-        offset = offset + jnp.where(iota((8, 1), 0) > h, through[h:h + 1, LANES - 1:], 0.0)
-    through = (through + offset).astype(I32)
-    counts = counts.astype(I32)
-    ends[0] = jnp.where(counts > 0, through - 1, TRADES)
-    ends[1] = jnp.where((through - counts < HALF) & (through > HALF), HALF - 1, TRADES)
+    upto = [jnp.zeros((8, LANES), I32) for _ in range(SETS // LANES)]
+    for c in range(LANES):
+        for v in range(4):
+            sets = jnp.broadcast_to(set_s[v][:, c:c + 1], (8, LANES))
+            upto = [u + jnp.where(sets <= lane + b * LANES, 1, 0) for b, u in enumerate(upto)]
+    for step in (4, 2, 1):
+        upto = [u + pltpu.roll(u, step, 0) for u in upto]
+    through = jnp.zeros((8, LANES), I32)
+    start = jnp.zeros((8, LANES), I32)
+    for b, u in enumerate(upto):
+        through = jnp.where(sub == b, u, through)
+        first = pltpu.roll(upto[b - 1], 1, 1) if b else jnp.zeros((8, LANES), I32)
+        start = jnp.where(sub == b, jnp.where(lane == 0, first, pltpu.roll(u, 1, 1)), start)
+    ends[0] = jnp.where(through > start, through - 1, TRADES)
+    ends[1] = jnp.where((start < HALF) & (through > HALF), HALF - 1, TRADES)
     to_ends = pltpu.make_async_copy(ends, ends_in, ends_sem)
     to_ends.start()
 
     spots = jnp.concatenate([spot_in[...], jnp.zeros((1, LANES - factors), F32)], axis=1)
     level = jnp.transpose(jnp.broadcast_to(spots, (LANES, LANES)))[:64]
     nets[TRADES] = jnp.zeros((dates, LANES), F32)
-
-    total = y_sum[...]
-    for i, copy in enumerate(to_z):
+    floors[TRADES] = jnp.zeros((1, LANES), F32)
+
+    def some_floors(c, accs):
+        accs = list(accs)
+        for j in range(32):
+            row = (j & 3) * 8 + (j >> 2)
+            for half in range(2):
+                column = c + half * (LANES // 2)
+                at = pl.ds(column * 32 + row, 1)
+                accs[half] = accs[half] * keeps[at, :] + notionals[at, :] * strikes[at, :]
+                floors[column * 32 + j] = accs[half]
+        return tuple(accs)
+
+    none = jnp.zeros((1, LANES), F32)
+    lax.fori_loop(0, LANES // 2, some_floors, (none, none))
+
+    to_x = []
+    for c in range(CHUNKS):
+        total = y_sum[part(c), :]
+        for i, copy in enumerate(to_z[c]):
+            copy.wait_recv()
+            total = total + over_z[i, part(c), :]
+        blocks[section, part(c), :] = total
+        to_x.append(
+            sends(x_peers, blocks.at[section], lambda i: blocks.at[section], x_send, x_recv, c)
+        )
+
+    own.wait()
+    for copy in to_d:
         copy.wait_recv()
-        total = total + over_z[i]
-    blocks[section] = total
-    to_x = [
-        remote(blocks.at[section], blocks.at[section], x_send.at[i], x_recv.at[i], peer)
-        for i, peer in enumerate(x_peers)
-    ]
-    for copy in to_x:
-        copy.start()
-    own.wait()
+    for e in range(sections):
+        for d in range(2):
+            high, rest = (part.astype(jnp.bfloat16) for part in halves(z_all[e, :, d, :]))
+            z_parts[2 * e + d] = jnp.concatenate([high, high, rest, rest], axis=0)
+
     to_order.wait()
     to_ends.wait()
-    for copy in to_d:
-        copy.wait_recv()
-    for copy in to_x:
-        copy.wait_recv()
+    for copies in to_x:
+        for copy in copies:
+            copy.wait_recv()
 
     for e in range(sections):
         for d, lower in enumerate(unpacked(blocks[e])):
+            high, rest = halves(lower)
+            both = (high + pltpu.roll(rest, 64, 1)).astype(jnp.bfloat16)
             level = level + jnp.dot(
-                lower[:, :64], z_all[e, d], precision=HIGHEST, preferred_element_type=F32
+                jnp.concatenate([both, both], axis=1), z_parts[2 * e + d], preferred_element_type=F32
             )
             prices[:, 2 * e + d, :] = jnp.exp(level)
 
@@ -249,9 +280,9 @@
             for half in range(2):
                 column = c + half * (LANES // 2)
                 at = pl.ds(column * 32 + row, 1)
-                price = prices[order_in[row, column]]
-                payoff = notionals[at, :] * jnp.maximum(price - strikes[at, :], 0.0)
-                accs[half] = accs[half] * keeps[at, :] + payoff
+                price = prices[order_in[column, row]]
+                above = notionals[at, :] * jnp.maximum(price, strikes[at, :])
+                accs[half] = accs[half] * keeps[at, :] + above
                 nets[column * 32 + j] = accs[half]
         return tuple(accs)
 
@@ -259,18 +290,14 @@
     lax.fori_loop(0, LANES // 2, some_trades, (zero, zero))
 
     lanes = iota((dates, LANES), 1)
-    step = 32
     for b in range(SETS // LANES):
-        def some_sets(q, sums_b):
-            for i in range(step):
-                at = q * step + i
-                last, halfway = (jnp.clip(ends_in[a, b, at], 0, TRADES) for a in range(2))
-                net = nets[last] + nets[halfway]
-                sum_s = jnp.sum(jnp.maximum(net, 0.0), axis=1, keepdims=True)
-                sums_b = jnp.where(lanes == at, sum_s, sums_b)
-            return sums_b
-
-        sums_b = lax.fori_loop(0, LANES // step, some_sets, jnp.zeros((dates, LANES), F32))
+        sums_b = jnp.zeros((dates, LANES), F32)
+        for at in range(LANES):
+            last, halfway = ends_in[0, b, at], ends_in[1, b, at]
+            floor = floors[last] + floors[halfway]
+            net = nets[last] + nets[halfway] - floor
+            sum_s = jnp.sum(jnp.maximum(net, 0.0), axis=1, keepdims=True)
+            sums_b = jnp.where(lanes == at, sum_s, sums_b)
         for d in range(dates):
             sums[4 * d + b:4 * d + b + 1, :] = sums_b[d:d + 1]
 
@@ -307,8 +334,12 @@
     for i, copy in enumerate(to_fz):
         copy.wait_recv()
         total = total + over_fz[i]
-    out[...] = total
-    for copies in (to_y, to_z, to_x, to_d, to_fx, to_fy, to_fz):
+    total = total / paths
+    for d in range(2):
+        for b in range(SETS // LANES):
+            at = d * (SETS // LANES) + b
+            out[d:d + 1, b * LANES:(b + 1) * LANES] = total[at:at + 1]
+    for copies in (*to_y, *to_z, *to_x, to_d, to_fx, to_fy, to_fz):
         for copy in copies:
             copy.wait_send()
 
@@ -319,13 +350,14 @@
     dma = pltpu.SemaphoreType.DMA
     vmem = pltpu.VMEM
     square = (ROWS, LANES)
-    totals = pl.pallas_call(
-        functools.partial(kernel, sections, ys, zs, factors),
-        out_shape=jax.ShapeDtypeStruct((8, LANES), F32),
+    paths = normal_draws.shape[2] * ys * zs
+    return pl.pallas_call(
+        functools.partial(kernel, sections, ys, zs, factors, paths),
+        out_shape=jax.ShapeDtypeStruct((2, SETS), F32),
         in_specs=[pl.BlockSpec(memory_space=pl.ANY)] * 8,
         out_specs=pl.BlockSpec(memory_space=pltpu.VMEM),
         scratch_shapes=[
-            vmem((2, factors, factors), F32),
+            vmem((2, factors, 1, factors), F32),
             vmem((1, factors), F32),
             pltpu.SMEM((dates,), I32),
             vmem((2, *square), I32),
@@ -337,15 +369,17 @@
             vmem((32, LANES), F32),
             vmem((zs - 1, 32, LANES), F32),
             vmem((sections, 32, LANES), F32),
-            vmem((sections, 2, 64, LANES), F32),
+            vmem((sections, 64, 2, LANES), F32),
+            vmem((dates, 256, LANES), jnp.bfloat16),
             vmem((64, dates, LANES), F32),
-            vmem(square, I32),
-            pltpu.SMEM(square, I32),
+            vmem((LANES, LANES), I32),
+            pltpu.SMEM((LANES, LANES), I32),
             vmem((2, 8, LANES), I32),
             pltpu.SMEM((2, 8, LANES), I32),
             vmem((TRADES, LANES), F32),
             vmem((TRADES, LANES), F32),
             vmem((TRADES, LANES), F32),
+            vmem((TRADES + 1, 1, LANES), F32),
             vmem((TRADES + 1, dates, LANES), F32),
             vmem((4 * dates, LANES), F32),
             vmem((sections - 1, 8, LANES), F32),
@@ -354,8 +388,9 @@
             vmem((8, LANES), F32),
             vmem((zs - 1, 8, LANES), F32),
             dma((7,)), dma, dma, dma,
-            dma((ys - 1,)), dma((ys - 1,)), dma((zs - 1,)), dma((zs - 1,)),
-            dma((sections - 1,)), dma((sections - 1,)), dma((sections - 1,)), dma((sections - 1,)),
+            dma((ys - 1, CHUNKS)), dma((ys - 1, CHUNKS)), dma((zs - 1, CHUNKS)), dma((zs - 1, CHUNKS)),
+            dma((sections - 1, CHUNKS)), dma((sections - 1, CHUNKS)),
+            dma((sections - 1,)), dma((sections - 1,)),
             dma((sections - 1,)), dma((sections - 1,)), dma((ys - 1,)), dma((ys - 1,)),
             dma((zs - 1,)), dma((zs - 1,)),
         ],
@@ -363,12 +398,10 @@
             collective_id=0, has_side_effects=True, vmem_limit_bytes=60 * 1024 * 1024
         ),
     )(
-        normal_draws, cholesky[:, 0], log_spot.reshape(1, factors), owner,
+        jnp.transpose(normal_draws, (1, 0, 2)), jnp.transpose(cholesky, (0, 2, 1, 3)), log_spot.reshape(1, factors), owner,
         trade_factor.reshape(square), trade_set.reshape(square),
         notional.reshape(square), strike.reshape(square),
     )
-    paths = normal_draws.shape[2] * ys * zs
-    return totals.reshape(2, SETS) / paths
 
 
 def solution(mesh):

time: 51.5 us -> 45.7 us (0.89)
  local copies, waits for them, and re-layouts: 4.06 us -> 1.28 us
  Pallas kernels: 46.5 us -> 44.2 us
  other arithmetic: 0.69 us -> 0 us
    pallas_call x1, Pallas kernels: 46.5 us -> 44.2 us  [shards(): pl.pallas_call(functools.partial(kernel, sections, ys, zs, factors, paths...]
    unnamed x2 -> x1, local copies, waits for them, and re-layouts: 2.84 us -> 1.28 us
    div x1 -> x0, other arithmetic: 0.69 us -> none  [shards(): return totals.reshape(2, SETS) / paths]
    squeeze x1 -> x0, local copies, waits for them, and re-layouts: 0.63 us -> none  [shards(): cholesky[:, 0]]
    div x1 -> x0, local copies, waits for them, and re-layouts: 0.6 us -> none  [shards(): return totals.reshape(2, SETS) / paths]
where the time goes in v1:
time: 45.7 us; the launch traced here: 45.5 us
  Pallas kernels  44.2 us (97%)
  local copies, waits for them, and re-layouts  1.28 us (3%)
    pallas_call x1, Pallas kernels, shards(): pl.pallas_call(functools.partial(kernel, sections, ys, zs, factors, paths...  44.2 us
    unnamed x1, local copies, waits for them, and re-layouts  1.28 us

profile of v1, /device:TPU:1, one launch (start us, length us, event | category | flops | bytes accessed | tf_op | source)
XLA Modules:
  0.0 45.5 jit_solution(8338969682968786213)
XLA Ops:
  0.0 44.2 %shard_map.82 = f32[2,512]{1,0:T(2,128)} custom-call(f32[60,2,1024]{2,1,0:T(2,128)} %bitcast.7, f32[2,60,1,60]{3,2,1,0:T(1,128)} %bitcast.8, f32[1,60]{1,0:T(1,128)} %bitcast.13, s32[16]{0:T(128)} %owner.1, s32[32,128]{1,0:T(8,128)} %bitcast.9, s32[32,128]{1,0:T(8,128)} %bitcast.10, f32[32,128]{1,0:T(8,128)} %bitcast.11, f32[32,128]{1,0:T(8,128)} %bitcast.12), custom_call_target="tpu_custom_call" | custom-call | tf_op jit(solution)/shard_map/pallas_call | solution.py:354
  44.3 1.3 %copy.10 = f32[2,512]{1,0:T(2,128)} copy(f32[2,512]{1,0:T(2,128)} %shard_map.82) | data formatting | bytes 8192

commit v2 on v1

--- a/solution.py
+++ b/solution.py
@@ -12,7 +12,7 @@
 LANES = 128
 ROWS = TRADES // LANES
 HALF = TRADES // 2
-CHUNKS = 2
+CHUNKS = 1
 MESH = pl.DeviceIdType.MESH
 HIGHEST = lax.Precision.HIGHEST
 F32 = jnp.float32
@@ -21,6 +21,10 @@
 
 def iota(shape, axis):
     return lax.broadcasted_iota(I32, shape, axis)
+
+
+def farthest_first(n):
+    return sorted(range(1, n), key=lambda i: -min(i, n - i))
 
 
 def remote(src, dst, send, recv, device):
@@ -94,7 +98,7 @@
     draws, chol, spot, owner, tfactor, tset, notional, strike, out,
     chol_in, spot_in, owner_in, trades_in, trades_f_in, pack_a, pack_b,
     mine, over_y, y_sum, over_z, blocks, z_all, z_parts, prices, order, order_in, ends, ends_in,
-    strikes, notionals, keeps, floors, nets, sums, over_x, x_sum, over_fy, fy_sum, over_fz,
+    strikes, notionals, keeps, nets, sums, over_x, x_sum, over_fy, fy_sum, over_fz,
     in_sems, order_sem, ends_sem, own_sem, y_send, y_recv, z_send, z_recv, x_send, x_recv,
     d_send, d_recv, fx_send, fx_recv, fy_send, fy_recv, fz_send, fz_recv,
 ):
@@ -102,12 +106,12 @@
     section = lax.axis_index("section")
     place = lax.axis_index("paths")
     y, z = lax.div(place, zs), lax.rem(place, zs)
-    y_peers = [(section, lax.rem(y + i, ys) * zs + z) for i in range(1, ys)]
-    z_peers = [(section, y * zs + lax.rem(z + i, zs)) for i in range(1, zs)]
-    x_peers = [(lax.rem(section + i, sections), place) for i in range(1, sections)]
+    y_peers = [(section, lax.rem(y + i, ys) * zs + z) for i in farthest_first(ys)]
+    z_peers = [(section, y * zs + lax.rem(z + i, zs)) for i in farthest_first(zs)]
+    x_peers = [(lax.rem(section + i, sections), place) for i in farthest_first(sections)]
 
     barrier = pltpu.get_barrier_semaphore()
-    for peer in y_peers + z_peers + x_peers:
+    for peer in z_peers + x_peers + y_peers:
         pl.semaphore_signal(barrier, inc=1, device_id=peer, device_id_type=MESH)
 
     loads = [
@@ -223,21 +227,6 @@
     spots = jnp.concatenate([spot_in[...], jnp.zeros((1, LANES - factors), F32)], axis=1)
     level = jnp.transpose(jnp.broadcast_to(spots, (LANES, LANES)))[:64]
     nets[TRADES] = jnp.zeros((dates, LANES), F32)
-    floors[TRADES] = jnp.zeros((1, LANES), F32)
-
-    def some_floors(c, accs):
-        accs = list(accs)
-        for j in range(32):
-            row = (j & 3) * 8 + (j >> 2)
-            for half in range(2):
-                column = c + half * (LANES // 2)
-                at = pl.ds(column * 32 + row, 1)
-                accs[half] = accs[half] * keeps[at, :] + notionals[at, :] * strikes[at, :]
-                floors[column * 32 + j] = accs[half]
-        return tuple(accs)
-
-    none = jnp.zeros((1, LANES), F32)
-    lax.fori_loop(0, LANES // 2, some_floors, (none, none))
 
     to_x = []
     for c in range(CHUNKS):
@@ -281,8 +270,8 @@
                 column = c + half * (LANES // 2)
                 at = pl.ds(column * 32 + row, 1)
                 price = prices[order_in[column, row]]
-                above = notionals[at, :] * jnp.maximum(price, strikes[at, :])
-                accs[half] = accs[half] * keeps[at, :] + above
+                payoff = notionals[at, :] * jnp.maximum(price - strikes[at, :], 0.0)
+                accs[half] = accs[half] * keeps[at, :] + payoff
                 nets[column * 32 + j] = accs[half]
         return tuple(accs)
 
@@ -294,8 +283,7 @@
         sums_b = jnp.zeros((dates, LANES), F32)
         for at in range(LANES):
             last, halfway = ends_in[0, b, at], ends_in[1, b, at]
-            floor = floors[last] + floors[halfway]
-            net = nets[last] + nets[halfway] - floor
+            net = nets[last] + nets[halfway]
             sum_s = jnp.sum(jnp.maximum(net, 0.0), axis=1, keepdims=True)
             sums_b = jnp.where(lanes == at, sum_s, sums_b)
         for d in range(dates):
@@ -379,7 +367,6 @@
             vmem((TRADES, LANES), F32),
             vmem((TRADES, LANES), F32),
             vmem((TRADES, LANES), F32),
-            vmem((TRADES + 1, 1, LANES), F32),
             vmem((TRADES + 1, dates, LANES), F32),
             vmem((4 * dates, LANES), F32),
             vmem((sections - 1, 8, LANES), F32),

time: 45.7 us -> 43.6 us (0.954)
  Pallas kernels: 44.2 us -> 42.2 us
    pallas_call x1, Pallas kernels: 44.2 us -> 42.2 us  [shards(): pl.pallas_call(functools.partial(kernel, sections, ys, zs, factors, paths...]
where the time goes in v2:
time: 43.6 us; the launch traced here: 43.5 us
  Pallas kernels  42.2 us (97%)
  local copies, waits for them, and re-layouts  1.28 us (3%)
    pallas_call x1, Pallas kernels, shards(): pl.pallas_call(functools.partial(kernel, sections, ys, zs, factors, paths...  42.2 us
    unnamed x1, local copies, waits for them, and re-layouts  1.28 us

profile of v2, /device:TPU:1, one launch (start us, length us, event | category | flops | bytes accessed | tf_op | source)
XLA Modules:
  0.0 43.5 jit_solution(16396885327013726754)
XLA Ops:
  0.0 42.2 %shard_map.82 = f32[2,512]{1,0:T(2,128)} custom-call(f32[60,2,1024]{2,1,0:T(2,128)} %bitcast.7, f32[2,60,1,60]{3,2,1,0:T(1,128)} %bitcast.8, f32[1,60]{1,0:T(1,128)} %bitcast.13, s32[16]{0:T(128)} %owner.1, s32[32,128]{1,0:T(8,128)} %bitcast.9, s32[32,128]{1,0:T(8,128)} %bitcast.10, f32[32,128]{1,0:T(8,128)} %bitcast.11, f32[32,128]{1,0:T(8,128)} %bitcast.12), custom_call_target="tpu_custom_call" | custom-call | tf_op jit(solution)/shard_map/pallas_call | solution.py:342
  42.2 1.3 %copy.10 = f32[2,512]{1,0:T(2,128)} copy(f32[2,512]{1,0:T(2,128)} %shard_map.82) | data formatting | bytes 8192

commit v3 on v2

--- a/solution.py
+++ b/solution.py
@@ -168,18 +168,6 @@
     for copy in to_d:
         copy.start()
 
-    for load in loads[2:]:
-        load.wait()
-    keys = [
-        trades_in[1, 8 * v:8 * v + 8, :] * 64 + trades_in[0, 8 * v:8 * v + 8, :] for v in range(4)
-    ]
-    carried = [[trades_f_in[a, 8 * v:8 * v + 8, :] for v in range(4)] for a in range(2)]
-    keys, (notional_s, strike_s) = in_set_order(keys, carried)
-    wide = jnp.concatenate([k & 63 for k in keys] * 4, axis=0)
-    order[...] = jnp.transpose(wide)
-    to_order = pltpu.make_async_copy(order, order_in, order_sem)
-    to_order.start()
-
     to_z = []
     for c in range(CHUNKS):
         total = mine[part(c), :]
@@ -188,6 +176,18 @@
             total = total + over_y[i, part(c), :]
         y_sum[part(c), :] = total
         to_z.append(sends(z_peers, y_sum, lambda i: over_z.at[i], z_send, z_recv, c))
+
+    for load in loads[2:]:
+        load.wait()
+    keys = [
+        trades_in[1, 8 * v:8 * v + 8, :] * 64 + trades_in[0, 8 * v:8 * v + 8, :] for v in range(4)
+    ]
+    carried = [[trades_f_in[a, 8 * v:8 * v + 8, :] for v in range(4)] for a in range(2)]
+    keys, (notional_s, strike_s) = in_set_order(keys, carried)
+    wide = jnp.concatenate([k & 63 for k in keys] * 4, axis=0)
+    order[...] = jnp.transpose(wide)
+    to_order = pltpu.make_async_copy(order, order_in, order_sem)
+    to_order.start()
 
     set_s = [k >> 6 for k in keys]
     sub, lane = iota((8, LANES), 0), iota((8, LANES), 1)
@@ -276,7 +276,7 @@
         return tuple(accs)
 
     zero = jnp.zeros((dates, LANES), F32)
-    lax.fori_loop(0, LANES // 2, some_trades, (zero, zero))
+    lax.fori_loop(0, LANES // 2, some_trades, (zero, zero), unroll=2)
 
     lanes = iota((dates, LANES), 1)
     for b in range(SETS // LANES):

time: 43.6 us -> 43.3 us (level)
  no operation moved by 1% of the time
where the time goes in v3:
time: 43.3 us; the launch traced here: 43.2 us
  Pallas kernels  41.9 us (97%)
  local copies, waits for them, and re-layouts  1.28 us (3%)
    pallas_call x1, Pallas kernels, shards(): pl.pallas_call(functools.partial(kernel, sections, ys, zs, factors, paths...  41.9 us
    unnamed x1, local copies, waits for them, and re-layouts  1.28 us

profile of v3, /device:TPU:1, one launch (start us, length us, event | category | flops | bytes accessed | tf_op | source)
XLA Modules:
  0.0 43.2 jit_solution(11476539570735943230)
XLA Ops:
  0.0 41.9 %shard_map.82 = f32[2,512]{1,0:T(2,128)} custom-call(f32[60,2,1024]{2,1,0:T(2,128)} %bitcast.7, f32[2,60,1,60]{3,2,1,0:T(1,128)} %bitcast.8, f32[1,60]{1,0:T(1,128)} %bitcast.13, s32[16]{0:T(128)} %owner.1, s32[32,128]{1,0:T(8,128)} %bitcast.9, s32[32,128]{1,0:T(8,128)} %bitcast.10, f32[32,128]{1,0:T(8,128)} %bitcast.11, f32[32,128]{1,0:T(8,128)} %bitcast.12), custom_call_target="tpu_custom_call" | custom-call | tf_op jit(solution)/shard_map/pallas_call | solution.py:342
  41.9 1.3 %copy.10 = f32[2,512]{1,0:T(2,128)} copy(f32[2,512]{1,0:T(2,128)} %shard_map.82) | data formatting | bytes 8192
